TPU v7x, 256 devices: a whole 4x4x8 slice. The times are simulated.
256 devices in a mesh: copy: 2 (over core), fsdp: 32 (over z, y), tp: 4 (over x).
Axes of the slice: x: 4, y: 4, z: 8, core: 2. Of those that a mesh axis runs over, the one named last changes fastest.
Arguments:
- gradients: float32 [256, 128, 4096], P('copy', 'fsdp', 'tp'), parts along dimension 0, may hold values from -6 to 6
- momentum: float32 [256, 128, 4096], P('copy', 'fsdp', 'tp'), parts along dimension 0, may hold values from -6 to 6
- weights: float32 [256, 128, 4096], P('copy', 'fsdp', 'tp'), parts along dimension 0, may hold values from -0.1875 to 0.1875
Outputs:
- new_weights: float32 [256, 128, 4096], P('copy', 'fsdp', 'tp'), parts along dimension 0
- new_momentum: float32 [256, 128, 4096], P('copy', 'fsdp', 'tp'), parts along dimension 0
There are 2 independent parts, one for each index of `copy`. A program takes and returns all parts, laid end to end along the dimension named above; each array names one. Nothing has to cross between parts.
All inputs are finite; a program needn't handle non-finite values.
Results may differ from a plain program's by a relative error of at most 0.00014.
Values sent between devices are 32-bit elements; how exact they have to be, the bound alone decides.
A program may use at most 64 MiB of HBM per device.

v0:
```python
import jax
import jax.numpy as jnp
from jax import lax
from jax.sharding import PartitionSpec as P

ITERS = 4
hold_rate = 0.95
learn_rate = 0.9
decay_rate = 0.1


def sent_to_all(x, axis):
    length = lax.axis_size(axis)
    return lax.all_to_all(jnp.broadcast_to(x[None], (length, *x.shape)), axis, 0, 0, tiled=True)


def taken_together(x, axis):
    return sent_to_all(x, axis).sum(axis=0)


def shards(gradients, momentum, weights):
    new_momentum = hold_rate * momentum + gradients
    direction = hold_rate * new_momentum + gradients
    moved = lax.all_to_all(direction, "fsdp", split_axis=0, concat_axis=1, tiled=True)
    total = lax.psum(jnp.sum(moved * moved, axis=(1, 2), keepdims=True), "tp")
    iterate = moved * lax.rsqrt(total + 1e-06)
    for step in range(ITERS):
        gram = taken_together(
            jnp.einsum("mik,mjk->mij", iterate, iterate, precision=lax.Precision.HIGHEST), "tp"
        )
        mixed = -4.775 * gram + 2.0315 * jnp.einsum(
            "mij,mjk->mik", gram, gram, precision=lax.Precision.HIGHEST
        )
        iterate = 3.4445 * iterate + jnp.einsum(
            "mij,mjk->mik", mixed, iterate, precision=lax.Precision.HIGHEST
        )
    back = lax.all_to_all(iterate, "fsdp", split_axis=1, concat_axis=0, tiled=True)
    new_weights = (1.0 - learn_rate * decay_rate) * weights - learn_rate * back
    return (new_weights, new_momentum)


def solution(mesh):
    return jax.shard_map(
        shards,
        mesh=mesh,
        in_specs=(P("copy", "fsdp", "tp"), P("copy", "fsdp", "tp"), P("copy", "fsdp", "tp")),
        out_specs=(P("copy", "fsdp", "tp"), P("copy", "fsdp", "tp")),
        check_vma=False,
    )
```

profile of v0, /device:TPU:8, one launch (start us, length us, event | category | flops | bytes accessed | tf_op | source)
XLA Modules:
  0.0 217.4 jit_solution(7391377207697536260)
XLA Ops:
  0.6 4.6 %multiply_add_fusion.4 = (f32[128,4,1024]{2,1,0:T(4,128)S(1)}, f32[128,4,1024]{2,1,0:T(4,128)}) fusion(f32[128,4,1024]{2,1,0:T(4,128)} %param.3, f32[128,4,1024]{2,1,0:T(4,128)} %param.4), kind=kLoop, calls=%fused_computation.7 | loop fusion | flops 2097152 | bytes 8388608 | tf_op jit(solution)/shard_map/add | solution.py:23
  5.3 62.0 %all_to_all.47 = f32[128,4,1024]{2,1,0:T(4,128)S(1)} all-to-all(f32[128,4,1024]{2,1,0:T(4,128)S(1)} %get-tuple-element.2), channel_id=1, replica_groups=mesh['copy'=2,'fsdp'=32,'tp'=4] {'fsdp'}, dimensions={0} | all-to-all | bytes 4194304 | tf_op jit(solution)/shard_map/all_to_all | solution.py:24
  67.3 0.6 multiply_reduce_fusion
  67.9 10.5 %psum.7 = f32[4,1,1]{0,2,1:T(1,128)S(1)} all-reduce(f32[4,1,1]{0,2,1:T(1,128)S(1)} %bitcast.38), channel_id=1, replica_groups=mesh['copy'=2,'fsdp'=32,'tp'=4] {'tp'}, use_global_device_ids=true, to_apply=%region_1.0 | all-reduce | flops 4 | bytes 32 | tf_op jit(solution)/shard_map/psum | solution.py:25
  78.4 1.5 copy_bitcast_fusion
  79.9 2.0 all_to_all.35
  81.9 0.0 copy-start.1
  81.9 2.3 %fusion.2 = f32[4,128,128]{2,1,0:T(8,128)S(1)} fusion(f32[4,128,1024]{2,1,0:T(8,128)S(1)} %all_to_all.35, f32[4]{0:T(128)S(1)} %rsqrt_bitcast_fusion), kind=kOutput, calls=%fused_computation.11 | convolution fusion | flops 805830656 | bytes 2359312 | tf_op jit(solution)/shard_map/mik,mjk->mij/dot_general | solution.py:29
  84.2 0.1 broadcast_in_dim.11
  84.3 14.1 %all_to_all.48 = f32[4,4,128,128]{3,2,1,0:T(8,128)S(1)} all-to-all(f32[4,4,128,128]{3,2,1,0:T(8,128)S(1)} %broadcast_in_dim.11), channel_id=1, replica_groups=mesh['copy'=2,'fsdp'=32,'tp'=4] {'tp'}, dimensions={0} | all-to-all | bytes 2097152 | tf_op jit(solution)/shard_map/all_to_all | solution.py:14
  98.4 0.0 copy-done.1
  98.4 0.1 reduce_sum.46
  98.5 0.4 fusion.9
  98.8 4.3 %multiply_add_fusion.3 = f32[4,128,1024]{2,1,0:T(8,128)S(1)} fusion(f32[4,128,1024]{2,1,0:T(8,128)} %copy-done.1, f32[4,128,128]{2,1,0:T(8,128)S(1)} %fusion.9, f32[4]{0:T(128)S(1)} %rsqrt_bitcast_fusion), kind=kOutput, calls=%fused_computation.5 | convolution fusion | flops 807403520 | bytes 4456464 | tf_op jit(solution)/shard_map/mij,mjk->mik/dot_general | solution.py:34
  103.1 2.0 fusion.12
  105.2 0.1 broadcast_in_dim.12
  105.3 13.3 %all_to_all.49 = f32[4,4,128,128]{3,2,1,0:T(8,128)S(1)} all-to-all(f32[4,4,128,128]{3,2,1,0:T(8,128)S(1)} %broadcast_in_dim.12), channel_id=1, replica_groups=mesh['copy'=2,'fsdp'=32,'tp'=4] {'tp'}, dimensions={0} | all-to-all | bytes 2097152 | tf_op jit(solution)/shard_map/all_to_all | solution.py:14
  118.6 0.1 reduce_sum.47
  118.7 0.4 fusion.8
  119.0 2.0 multiply_add_fusion.2
  121.1 0.0 copy-start
  121.1 2.0 fusion.13
  123.2 0.0 copy-done
  123.2 0.1 broadcast_in_dim.13
  123.3 13.3 %all_to_all.50 = f32[4,4,128,128]{3,2,1,0:T(8,128)S(1)} all-to-all(f32[4,4,128,128]{3,2,1,0:T(8,128)S(1)} %broadcast_in_dim.13), channel_id=1, replica_groups=mesh['copy'=2,'fsdp'=32,'tp'=4] {'tp'}, dimensions={0} | all-to-all | bytes 2097152 | tf_op jit(solution)/shard_map/all_to_all | solution.py:14
  136.6 0.1 reduce_sum.48
  136.7 0.4 fusion.7
  137.0 4.2 %multiply_add_fusion.1 = f32[4,128,1024]{2,1,0:T(8,128)S(1)} fusion(f32[4,128,1024]{2,1,0:T(8,128)} %copy-done, f32[4,128,128]{2,1,0:T(8,128)S(1)} %fusion.7), kind=kOutput, calls=%fused_computation.3 | convolution fusion | flops 806354944 | bytes 4456448 | tf_op jit(solution)/shard_map/mij,mjk->mik/dot_general | solution.py:34
  141.2 2.0 fusion.14
  143.3 0.1 broadcast_in_dim.14
  143.4 13.3 %all_to_all.51 = f32[4,4,128,128]{3,2,1,0:T(8,128)S(1)} all-to-all(f32[4,4,128,128]{3,2,1,0:T(8,128)S(1)} %broadcast_in_dim.14), channel_id=1, replica_groups=mesh['copy'=2,'fsdp'=32,'tp'=4] {'tp'}, dimensions={0} | all-to-all | bytes 2097152 | tf_op jit(solution)/shard_map/all_to_all | solution.py:14
  156.7 0.1 reduce_sum.49
  156.8 0.4 fusion.6
  157.1 2.0 multiply_add_fusion
  159.2 1.4 copy.11
  160.5 51.9 %all_to_all.52 = f32[4,128,1024]{2,0,1:T(4,128)S(1)} all-to-all(f32[4,128,1024]{2,0,1:T(4,128)S(1)} %copy.11), channel_id=1, replica_groups=mesh['copy'=2,'fsdp'=32,'tp'=4] {'fsdp'}, dimensions={1} | all-to-all | bytes 4194304 | tf_op jit(solution)/shard_map/all_to_all | solution.py:37
  212.4 0.7 broadcast_multiply_fusion
  213.1 0.0 copy-start.2
  213.1 1.8 copy.12
  214.9 0.0 copy-done.2
  214.9 2.5 %bitcast_subtract_fusion = f32[128,4,1024]{2,1,0:T(4,128)} fusion(f32[32,4,4,1024]{3,2,1,0:T(4,128)S(1)} %copy.12, f32[128,4,1024]{2,1,0:T(4,128)S(1)} %copy-done.2), kind=kLoop, calls=%fused_computation | loop fusion | flops 1048576 | bytes 6291456 | tf_op jit(solution)/shard_map/sub | solution.py:38
  (1 shorter events, 0.0 us)
Async XLA Ops:
  81.9 16.5 %copy-start.1 = (f32[4,128,1024]{2,1,0:T(8,128)}, f32[4,128,1024]{2,1,0:T(8,128)S(1)}, u32[]{:S(2)}) copy-start(f32[4,128,1024]{2,1,0:T(8,128)S(1)} %all_to_all.35) | copy-start | bytes 6291460
  121.1 2.1 copy-start
  213.1 1.8 copy-start.2
where the time goes:
time: 218 us; the launch traced here: 217 us
  blocking collectives  178 us (82%)
  matrix products  22.4 us (10%)
  other arithmetic  8.7 us (4%)
  local copies, waits for them, and re-layouts  7.09 us (3%)
    all_to_all x1, blocking collectives, shards(): lax.all_to_all(direction, 'fsdp', split_axis=0, concat_axis=1, tiled=True)  62 us
    all_to_all x4, blocking collectives, sent_to_all(): lax.all_to_all(jnp.broadcast_to(x[None], (length, *x.shape)), axis, 0, 0,...  54 us
    all_to_all x1, blocking collectives, shards(): lax.all_to_all(iterate, 'fsdp', split_axis=1, concat_axis=0, tiled=True)  51.9 us
    dot_general x4, matrix products, shards(): jnp.einsum('mij,mjk->mik', mixed, iterate, precision=lax.Precision.HIGHEST)  12.5 us
    psum x1, blocking collectives, shards(): total = lax.psum(jnp.sum(moved * moved, axis=(1, 2), keepdims=True), 'tp')  10.5 us
    dot_general x4, matrix products, shards(): jnp.einsum('mik,mjk->mij', iterate, iterate, precision=lax.Precision.HIGH...  8.4 us
    add x1, other arithmetic, shards(): direction = hold_rate * new_momentum + gradients  4.62 us

commit v1 on v0

--- a/solution.py
+++ b/solution.py
@@ -34,7 +34,10 @@
         iterate = 3.4445 * iterate + jnp.einsum(
             "mij,mjk->mik", mixed, iterate, precision=lax.Precision.HIGHEST
         )
-    back = lax.all_to_all(iterate, "fsdp", split_axis=1, concat_axis=0, tiled=True)
+    back = jnp.concatenate(
+        lax.all_to_all(jnp.stack(jnp.split(iterate, lax.axis_size("fsdp"), axis=1)), "fsdp", 0, 0),
+        axis=0,
+    )
     new_weights = (1.0 - learn_rate * decay_rate) * weights - learn_rate * back
     return (new_weights, new_momentum)
 

time: 218 us -> 216 us (level)
  no operation moved by 1% of the time
where the time goes in v1:
time: 216 us
  blocking collectives  178 us (82%)
  matrix products  22.4 us (10%)
  other arithmetic  8.6 us (4%)
  local copies, waits for them, and re-layouts  5.61 us (3%)
    all_to_all x1, blocking collectives, shards(): lax.all_to_all(direction, 'fsdp', split_axis=0, concat_axis=1, tiled=True)  62 us
    all_to_all x4, blocking collectives, sent_to_all(): lax.all_to_all(jnp.broadcast_to(x[None], (length, *x.shape)), axis, 0, 0,...  54 us
    all_to_all x1, blocking collectives, shards(): lax.all_to_all(jnp.stack(jnp.split(iterate, lax.axis_size('fsdp'), axis=1...  51.9 us
    dot_general x4, matrix products, shards(): jnp.einsum('mij,mjk->mik', mixed, iterate, precision=lax.Precision.HIGHEST)  12.5 us
    psum x1, blocking collectives, shards(): total = lax.psum(jnp.sum(moved * moved, axis=(1, 2), keepdims=True), 'tp')  10.5 us
    dot_general x4, matrix products, shards(): jnp.einsum('mik,mjk->mij', iterate, iterate, precision=lax.Precision.HIGH...  8.4 us
    add x1, other arithmetic, shards(): direction = hold_rate * new_momentum + gradients  4.62 us

profile of v1, /device:TPU:8, one launch (start us, length us, event | category | flops | bytes accessed | tf_op | source)
XLA Modules:
  0.0 216.0 jit_solution(4196963520418748703)
XLA Ops:
  0.6 4.6 %multiply_add_fusion.4 = (f32[128,4,1024]{2,1,0:T(4,128)S(1)}, f32[128,4,1024]{2,1,0:T(4,128)}) fusion(f32[128,4,1024]{2,1,0:T(4,128)} %param.3, f32[128,4,1024]{2,1,0:T(4,128)} %param.4), kind=kLoop, calls=%fused_computation.7 | loop fusion | flops 2097152 | bytes 8388608 | tf_op jit(solution)/shard_map/add | solution.py:23
  5.3 62.0 %all_to_all.43 = f32[128,4,1024]{2,1,0:T(4,128)S(1)} all-to-all(f32[128,4,1024]{2,1,0:T(4,128)S(1)} %get-tuple-element.2), channel_id=1, replica_groups=mesh['copy'=2,'fsdp'=32,'tp'=4] {'fsdp'}, dimensions={0} | all-to-all | bytes 4194304 | tf_op jit(solution)/shard_map/all_to_all | solution.py:24
  67.3 0.6 multiply_reduce_fusion
  67.9 10.5 %psum.7 = f32[4,1,1]{0,2,1:T(1,128)S(1)} all-reduce(f32[4,1,1]{0,2,1:T(1,128)S(1)} %bitcast.162), channel_id=1, replica_groups=mesh['copy'=2,'fsdp'=32,'tp'=4] {'tp'}, use_global_device_ids=true, to_apply=%region_1.0 | all-reduce | flops 4 | bytes 32 | tf_op jit(solution)/shard_map/psum | solution.py:25
  78.4 1.5 copy_bitcast_fusion
  79.9 2.0 all_to_all.31
  81.9 0.0 copy-start.1
  81.9 2.3 %fusion.2 = f32[4,128,128]{2,1,0:T(8,128)S(1)} fusion(f32[4,128,1024]{2,1,0:T(8,128)S(1)} %all_to_all.31, f32[4]{0:T(128)S(1)} %rsqrt_bitcast_fusion), kind=kOutput, calls=%fused_computation.11 | convolution fusion | flops 805830656 | bytes 2359312 | tf_op jit(solution)/shard_map/mik,mjk->mij/dot_general | solution.py:29
  84.2 0.1 broadcast_in_dim.11
  84.3 14.1 %all_to_all.44 = f32[4,4,128,128]{3,2,1,0:T(8,128)S(1)} all-to-all(f32[4,4,128,128]{3,2,1,0:T(8,128)S(1)} %broadcast_in_dim.11), channel_id=1, replica_groups=mesh['copy'=2,'fsdp'=32,'tp'=4] {'tp'}, dimensions={0} | all-to-all | bytes 2097152 | tf_op jit(solution)/shard_map/all_to_all | solution.py:14
  98.4 0.0 copy-done.1
  98.4 0.1 reduce_sum.46
  98.5 0.4 fusion.9
  98.8 4.3 %multiply_add_fusion.3 = f32[4,128,1024]{2,1,0:T(8,128)S(1)} fusion(f32[4,128,1024]{2,1,0:T(8,128)} %copy-done.1, f32[4,128,128]{2,1,0:T(8,128)S(1)} %fusion.9, f32[4]{0:T(128)S(1)} %rsqrt_bitcast_fusion), kind=kOutput, calls=%fused_computation.5 | convolution fusion | flops 807403520 | bytes 4456464 | tf_op jit(solution)/shard_map/mij,mjk->mik/dot_general | solution.py:34
  103.1 2.0 fusion.12
  105.2 0.1 broadcast_in_dim.12
  105.3 13.3 %all_to_all.45 = f32[4,4,128,128]{3,2,1,0:T(8,128)S(1)} all-to-all(f32[4,4,128,128]{3,2,1,0:T(8,128)S(1)} %broadcast_in_dim.12), channel_id=1, replica_groups=mesh['copy'=2,'fsdp'=32,'tp'=4] {'tp'}, dimensions={0} | all-to-all | bytes 2097152 | tf_op jit(solution)/shard_map/all_to_all | solution.py:14
  118.6 0.1 reduce_sum.47
  118.7 0.4 fusion.8
  119.0 2.0 multiply_add_fusion.2
  121.1 0.0 copy-start
  121.1 2.0 fusion.13
  123.2 0.0 copy-done
  123.2 0.1 broadcast_in_dim.13
  123.3 13.3 %all_to_all.46 = f32[4,4,128,128]{3,2,1,0:T(8,128)S(1)} all-to-all(f32[4,4,128,128]{3,2,1,0:T(8,128)S(1)} %broadcast_in_dim.13), channel_id=1, replica_groups=mesh['copy'=2,'fsdp'=32,'tp'=4] {'tp'}, dimensions={0} | all-to-all | bytes 2097152 | tf_op jit(solution)/shard_map/all_to_all | solution.py:14
  136.6 0.1 reduce_sum.48
  136.7 0.4 fusion.7
  137.0 4.2 %multiply_add_fusion.1 = f32[4,128,1024]{2,1,0:T(8,128)S(1)} fusion(f32[4,128,1024]{2,1,0:T(8,128)} %copy-done, f32[4,128,128]{2,1,0:T(8,128)S(1)} %fusion.7), kind=kOutput, calls=%fused_computation.3 | convolution fusion | flops 806354944 | bytes 4456448 | tf_op jit(solution)/shard_map/mij,mjk->mik/dot_general | solution.py:34
  141.2 2.0 fusion.14
  143.3 0.1 broadcast_in_dim.14
  143.4 13.3 %all_to_all.47 = f32[4,4,128,128]{3,2,1,0:T(8,128)S(1)} all-to-all(f32[4,4,128,128]{3,2,1,0:T(8,128)S(1)} %broadcast_in_dim.14), channel_id=1, replica_groups=mesh['copy'=2,'fsdp'=32,'tp'=4] {'tp'}, dimensions={0} | all-to-all | bytes 2097152 | tf_op jit(solution)/shard_map/all_to_all | solution.py:14
  156.7 0.1 reduce_sum.49
  156.8 0.4 fusion.6
  157.1 2.0 multiply_add_fusion
  160.0 51.9 %all_to_all.48 = f32[32,4,4,1024]{3,2,1,0:T(4,128)S(1)} all-to-all(f32[32,4,4,1024]{3,2,1,0:T(4,128)S(1)} %constant_dynamic-update-slice_fusion), channel_id=1, replica_groups=mesh['copy'=2,'fsdp'=32,'tp'=4] {'fsdp'}, dimensions={0} | all-to-all | bytes 4194304 | tf_op jit(solution)/shard_map/all_to_all | solution.py:38
  211.9 0.0 copy-start.2
  211.9 0.6 broadcast_multiply_fusion
  212.5 1.0 copy-done.2
  213.5 2.5 %bitcast_subtract_fusion = f32[128,4,1024]{2,1,0:T(4,128)} fusion(f32[32,4,4,1024]{3,2,1,0:T(4,128)S(1)} %broadcast_multiply_fusion, f32[128,4,1024]{2,1,0:T(4,128)S(1)} %copy-done.2), kind=kLoop, calls=%fused_computation | loop fusion | flops 1048576 | bytes 6291456 | tf_op jit(solution)/shard_map/sub | solution.py:41
  (33 shorter events, 0.7 us)
Async XLA Ops:
  81.9 16.5 %copy-start.1 = (f32[4,128,1024]{2,1,0:T(8,128)}, f32[4,128,1024]{2,1,0:T(8,128)S(1)}, u32[]{:S(2)}) copy-start(f32[4,128,1024]{2,1,0:T(8,128)S(1)} %all_to_all.31) | copy-start | bytes 6291460
  121.1 2.1 copy-start
  211.9 1.6 copy-start.2
